TPU v7x, 256 devices: a whole 4x4x8 slice. The times are simulated.
256 devices in a mesh: lb: 8 (over z), rb: 16 (over x, y), wa: 2 (over core).
Axes of the slice: x: 4, y: 4, z: 8, core: 2. Of those that a mesh axis runs over, the one named last changes fastest.
Arguments:
- initial_guess: bfloat16 [8192, 4, 128], P(('lb', 'rb')), may hold values from -6 to 6
- left_environment: bfloat16 [8, 8, 16, 64, 8192], P('wa', None, 'rb', None, 'lb'), may hold values from -12 to 12, as said below
- right_environment: bfloat16 [128, 8, 128], replicated, may hold values from -12 to 12, as said below
- operator_blocks: float32 [16, 4, 4], replicated, may hold values from -4 to 4
- operator_pairs: int32 [16, 2], replicated, may hold values from 0 to 7
Outputs:
- ritz_vector: float32 [8192, 4, 128], P(('lb', 'rb'))
- residual: float32 [8192, 4, 128], P(('lb', 'rb'))
Inputs may be any that keep to these rules, and one draw needn't show every extreme that they name: `operator_pairs`: each row names the left and the right MPO index of one operator block; blocks with the same pair add. `left_environment`: for each MPO index the [8192, 8192] matrix is symmetric. `right_environment`: for each MPO index the matrix over the two right bond states is symmetric.
All inputs are finite; a program needn't handle non-finite values.
Results may differ from a plain program's by a relative error of at most 0.014.
Values may be sent and summed in bfloat16 or wider, within the bound.
A program may use at most 128 MiB of HBM per device.

v0:
```python
import functools

import jax
import jax.numpy as jnp
from jax import lax
from jax.experimental import pallas as pl
from jax.experimental.pallas import tpu as pltpu
from jax.sharding import PartitionSpec as P

ITERS = 3
SWEEPS = 8

highest = lax.Precision.HIGHEST
epsilon = 1e-06

TILE = (8, 128)
MESH = pl.DeviceIdType.MESH


def half_angle(y, x):
    scale = jnp.maximum(jnp.abs(x), jnp.abs(y))
    zero = scale == 0.0
    inverse = 1.0 / jnp.where(zero, 1.0, scale)
    xs, ys = x * inverse, y * inverse
    h = jnp.sqrt(xs * xs + ys * ys)
    h = jnp.where(zero, 1.0, h)
    big = jnp.sqrt(0.5 * (1.0 + jnp.abs(xs) / h))
    small = 0.5 * jnp.abs(ys) / (h * big)
    positive = x >= 0.0
    cosine = jnp.where(positive, big, small)
    sine = jnp.where(positive, small, big) * jnp.where(y < 0.0, -1.0, 1.0)
    return jnp.where(zero, 1.0, cosine), jnp.where(zero, 0.0, sine)


def lowest(entries, order):
    one, none = jnp.full(TILE, 1.0, jnp.float32), jnp.full(TILE, 0.0, jnp.float32)
    if order == 1:
        return entries[(0, 0)], [one]

    def at(i, j):
        return (min(i, j), max(i, j))

    keys = [(i, j) for i in range(order) for j in range(i, order)]
    start = tuple(entries[key] for key in keys)
    vectors0 = tuple(one if i == j else none for i in range(order) for j in range(order))

    def sweep(_, carry):
        m = dict(zip(keys, carry[0]))
        v = list(carry[1])
        for p in range(order):
            for q in range(p + 1, order):
                a, b, d = m[(p, p)], m[(p, q)], m[(q, q)]
                c, s = half_angle(2.0 * b, d - a)
                m[(p, p)] = c * (c * a - s * b) - s * (c * b - s * d)
                m[(p, q)] = s * (c * a - s * b) + c * (c * b - s * d)
                m[(q, q)] = s * (s * a + c * b) + c * (s * b + c * d)
                for i in range(order):
                    if i != p and i != q:
                        x, y = m[at(i, p)], m[at(i, q)]
                        m[at(i, p)] = c * x - s * y
                        m[at(i, q)] = s * x + c * y
                    x, y = v[i * order + p], v[i * order + q]
                    v[i * order + p] = c * x - s * y
                    v[i * order + q] = s * x + c * y
        return tuple(m[key] for key in keys), tuple(v)

    values, vectors = lax.fori_loop(0, SWEEPS, sweep, (start, vectors0))
    m = dict(zip(keys, values))
    best = m[(0, 0)]
    weights = [vectors[i * order] for i in range(order)]
    for j in range(1, order):
        better = m[(j, j)] < best
        best = jnp.where(better, m[(j, j)], best)
        weights = [jnp.where(better, vectors[i * order + j], weights[i]) for i in range(order)]
    sign = jnp.where(weights[0] < 0.0, -1.0, 1.0)
    return best, [weight * sign for weight in weights]


def tiled(value, rows, columns):
    wide = jnp.concatenate([value] * (columns // 128), axis=1)
    return jnp.concatenate([wide] * (rows // 8), axis=0)


def wait_bytes(ref, sem):
    pltpu.make_async_copy(ref, ref, sem).wait()


def far_first(size):
    steps = list(range(size))
    return sorted(steps, key=lambda step: -min(step, size - step))


def davidson_kernel(sizes, guess_ref, left_hbm, joint_ref, level_ref, ritz_ref, residual_ref,
                    lv, x, y, y_own, z, part, swap_out, swap_in, rs_out, rs_in,
                    dl_mine, dl_swap, dl_all, diag, coef, sc_xy, sc_z,
                    left_sem, gather_send, gather_recv, fwd_send, fwd_recv,
                    xy_send, xy_recv, z_send, z_recv, swap_send, swap_recv,
                    rs_send, rs_recv, out_send, out_recv):
    lb, rb, wa, side, half, width, levels, total_count = sizes
    own = 2 * half
    li, ri, wi = lax.axis_index("lb"), lax.axis_index("rb"), lax.axis_index("wa")
    other = 1 - wi
    xi, yi = ri // side, ri % side
    mine = ri * 2 + wi
    order = far_first(lb)
    group = lb // 2

    def plane_peer(step):
        return ((xi + step // side) % side) * side + (yi + step % side) % side

    def plane_source(step):
        return ((xi + side - step // side) % side) * side + (yi + side - step % side) % side

    for place, step in enumerate(order):
        pltpu.make_async_copy(
            left_hbm.at[:, (li + step) % lb], lv.at[:, place], left_sem.at[place]
        ).start()

    barrier = pltpu.get_barrier_semaphore()

    def greet_plane(step, carry):
        pl.semaphore_signal(barrier, inc=1, device_id={"rb": plane_peer(step)}, device_id_type=MESH)
        return carry

    lax.fori_loop(1, rb, greet_plane, 0)

    def greet_column(step, carry):
        pl.semaphore_signal(
            barrier, inc=1,
            device_id={"lb": (li + step // 2) % lb, "wa": (wi + step) % 2},
            device_id_type=MESH,
        )
        return carry

    lax.fori_loop(1, 2 * lb, greet_column, 0)
    pl.semaphore_wait(barrier, rb - 1 + 2 * lb - 1)

    def gather_start(number, source, buf):
        def send(index, carry):
            step = rb - 1 - index
            pltpu.make_async_remote_copy(
                src_ref=source, dst_ref=buf.at[mine],
                send_sem=gather_send.at[number], recv_sem=gather_recv.at[number, step],
                device_id={"rb": plane_peer(step)}, device_id_type=MESH,
            ).start()
            return carry

        lax.fori_loop(0, rb - 1, send, 0)

    def forward(number, source, buf, slot):
        pltpu.make_async_remote_copy(
            src_ref=source, dst_ref=buf.at[slot],
            send_sem=fwd_send.at[number], recv_sem=fwd_recv.at[number],
            device_id={"wa": other}, device_id_type=MESH,
        ).start()

    def gather_forward(number, buf):
        def step_body(index, carry):
            step = rb - 1 - index
            slot = plane_source(step) * 2 + wi
            wait_bytes(buf.at[slot], gather_recv.at[number, step])
            forward(number, buf.at[slot], buf, slot)
            return carry

        lax.fori_loop(0, rb - 1, step_body, 0)

    def gather_finish(number, buf, count):
        wait_bytes(buf.at[pl.ds(0, count)], fwd_recv.at[number])
        wait_bytes(buf.at[pl.ds(0, count)], fwd_send.at[number])
        wait_bytes(buf.at[pl.ds(0, rb - 1)], gather_send.at[number])

    gather_start(0, guess_ref.at[wi], x.at[0])
    x[0, ri * 2] = guess_ref[0]
    x[0, ri * 2 + 1] = guess_ref[1]

    for place, step in enumerate(order):
        wait_bytes(lv.at[:, place], left_sem.at[place])
    per_tile = 128 // own
    lane = lax.broadcasted_iota(jnp.int32, (own, 128), 1)
    row = lax.broadcasted_iota(jnp.int32, (own, 128), 0)
    hit = lane == row + (ri % per_tile) * own
    entries = jnp.zeros((own, 128), jnp.float32)
    for level in range(levels // 2):
        block = lv[level, order.index(0), :, pl.ds(pl.multiple_of((ri // per_tile) * 128, 128), 128)]
        column = jnp.sum(jnp.where(hit, block.astype(jnp.float32), 0.0), axis=1, keepdims=True)
        entries = entries + jnp.where(lane == wi * (levels // 2) + level, column, 0.0)
    dl_mine[...] = entries.astype(jnp.bfloat16)
    swap_diag = pltpu.make_async_remote_copy(
        src_ref=dl_mine, dst_ref=dl_swap, send_sem=out_send.at[2], recv_sem=out_recv.at[2],
        device_id={"wa": other}, device_id_type=MESH,
    )
    swap_diag.start()
    gather_forward(0, x.at[0])
    swap_diag.wait()
    both = (dl_mine[...].astype(jnp.float32) + dl_swap[...].astype(jnp.float32)).astype(jnp.bfloat16)
    dl_all[ri * 2] = both[:half]
    dl_all[ri * 2 + 1] = both[half:]
    gather_start(1, dl_all.at[mine], dl_all)
    gather_finish(0, x.at[0], rb - 1)

    gram, cross, mix = {}, {}, {}
    for k in range(ITERS + 1):
        def level_body(level, carry):
            product = jnp.dot(
                lv[level].reshape(lb * own, lb_depth), x[k].reshape(lb_depth, width),
                preferred_element_type=jnp.float32,
            )
            z[:, pl.ds(pl.multiple_of(level * width, 128), width)] = product.astype(jnp.bfloat16)
            return carry

        lb_depth = rb * own
        lax.fori_loop(0, levels // 2, level_body, 0)

        def swap_copy(turn):
            rows = pl.ds(turn * group, group)
            return pltpu.make_async_remote_copy(
                src_ref=swap_out.at[rows], dst_ref=swap_in.at[rows],
                send_sem=swap_send.at[k, turn], recv_sem=swap_recv.at[k, turn],
                device_id={"wa": other}, device_id_type=MESH,
            )

        for turn in range(2):
            rows = pl.ds(turn * group * own, group * own)
            product = jnp.dot(z[rows], joint_ref[...], preferred_element_type=jnp.float32)
            part[pl.ds(turn * group, group)] = product.reshape(group, 2, half, width)
            for place in range(turn * group, (turn + 1) * group):
                swap_out[place] = part[place, other].astype(jnp.bfloat16)
            swap_copy(turn).start()

        for turn in range(2):
            swap_copy(turn).wait()
            for place in range(turn * group, (turn + 1) * group):
                step = order[place]
                if step == 0:
                    continue
                total = part[place, wi] + swap_in[place].astype(jnp.float32)
                rs_out[place] = total.astype(jnp.bfloat16)
                pltpu.make_async_remote_copy(
                    src_ref=rs_out.at[place], dst_ref=rs_in.at[place],
                    send_sem=rs_send.at[k], recv_sem=rs_recv.at[k],
                    device_id={"lb": (li + step) % lb}, device_id_type=MESH,
                ).start()
        last = order.index(0)
        image = part[last, wi] + swap_in[last].astype(jnp.float32)
        if k == 0:
            gather_forward(1, dl_all)
        wait_bytes(rs_in.at[pl.ds(0, lb - 1)], rs_recv.at[k])
        for place in range(lb - 1):
            image = image + rs_in[place].astype(jnp.float32)
        y_own[k] = image
        if k < ITERS:
            y[k, mine] = image.astype(jnp.bfloat16)

        vector = x[k, mine].astype(jnp.float32)
        rows = []

        def products(first, second):
            line = jnp.sum(first * second, axis=0, keepdims=True)
            folded = line[:, :128]
            for column in range(1, width // 128):
                folded = folded + line[:, column * 128 : (column + 1) * 128]
            return folded

        for j in range(k + 1):
            rows.append(products(x[j, mine].astype(jnp.float32), vector))
        for j in range(k + 1):
            rows.append(products(x[j, mine].astype(jnp.float32), image))
        rows += [jnp.zeros((1, 128), jnp.float32)] * (8 - len(rows))
        sc_xy[k, ri] = jnp.concatenate(rows, axis=0)

        def send_plane(index, carry):
            step = rb - 1 - index
            pltpu.make_async_remote_copy(
                src_ref=sc_xy.at[k, ri], dst_ref=sc_xy.at[k, ri],
                send_sem=xy_send.at[k], recv_sem=xy_recv.at[k],
                device_id={"rb": plane_peer(step)}, device_id_type=MESH,
            ).start()
            return carry

        lax.fori_loop(0, rb - 1, send_plane, 0)
        if k < ITERS:
            gather_start(2 + k, y.at[k, mine], y.at[k])
            forward(2 + k, y.at[k, mine], y.at[k], mine)
        wait_bytes(rs_out.at[pl.ds(0, lb - 1)], rs_send.at[k])
        wait_bytes(sc_xy.at[k, pl.ds(0, rb - 1)], xy_recv.at[k])
        summed = sc_xy[k, 0]
        for j in range(1, rb):
            summed = summed + sc_xy[k, j]
        column_mine = li * 2 + wi
        sc_z[k, column_mine] = summed

        def send_column(step, carry):
            pltpu.make_async_remote_copy(
                src_ref=sc_z.at[k, column_mine], dst_ref=sc_z.at[k, column_mine],
                send_sem=z_send.at[k], recv_sem=z_recv.at[k],
                device_id={"lb": (li + step // 2) % lb, "wa": (wi + step) % 2},
                device_id_type=MESH,
            ).start()
            return carry

        lax.fori_loop(1, 2 * lb, send_column, 0)
        if k < ITERS:
            gather_forward(2 + k, y.at[k])
        if k == 0:
            gather_finish(1, dl_all, rb - 1)
            lines = dl_all[...].reshape(2 * rb * half, 128)
            rest = level_ref[...]
            found = jnp.zeros((2 * rb * half, width), jnp.float32)
            for _ in range(3):
                term = rest.astype(jnp.bfloat16)
                rest = rest - term.astype(jnp.float32)
                found = found + jnp.dot(lines, term, preferred_element_type=jnp.float32)
            diag[...] = found.reshape(2 * rb, half, width)
        wait_bytes(sc_z.at[k, pl.ds(0, 2 * lb - 1)], z_recv.at[k])
        total = sc_z[k, 0]
        for j in range(1, 2 * lb):
            total = total + sc_z[k, j]
        total = jnp.sum(total, axis=1, keepdims=True) * (1.0 / total_count)
        scalars = [jnp.broadcast_to(total[q : q + 1], TILE) for q in range(2 * k + 2)]
        for j in range(k + 1):
            gram[(j, k)] = gram[(k, j)] = scalars[j]
            cross[(j, k)] = cross[(k, j)] = scalars[k + 1 + j]
        raw = [jnp.zeros(TILE, jnp.float32) for _ in range(k)] + [jnp.ones(TILE, jnp.float32)]
        for j in range(k):
            correlation = sum(mix[(j, i)] * gram[(i, k)] for i in range(j + 1))
            for i in range(j + 1):
                raw[i] = raw[i] - correlation * mix[(j, i)]
        norm = jnp.zeros(TILE, jnp.float32)
        for i in range(k + 1):
            norm = norm + raw[i] * sum(raw[j] * gram[(i, j)] for j in range(k + 1))
        scale = lax.rsqrt(jnp.maximum(norm, 0.0) + epsilon)
        for i in range(k + 1):
            mix[(k, i)] = raw[i] * scale
        entries = {}
        for b in range(k + 1):
            image_row = [
                sum(mix[(b, j)] * cross[(i, j)] for j in range(b + 1)) for i in range(b + 1)
            ]
            for a in range(b + 1):
                entries[(a, b)] = sum(mix[(a, i)] * image_row[i] for i in range(a + 1))
        theta, weights = lowest(entries, k + 1)
        alphas = [
            sum(weights[j] * mix[(j, i)] for j in range(i, k + 1)) for i in range(k + 1)
        ]
        for i in range(k + 1):
            coef[i] = alphas[i]
            coef[4 + i] = -(theta * alphas[i])
        coef[8] = theta

        if k < ITERS:
            gather_finish(2 + k, y.at[k], rb)

            def correct(chunk, carry):
                for start in range(0, half, 16):
                    span = pl.ds(start, 16)
                    ritz = tiled(coef[8], 16, width)
                    residual = jnp.zeros((16, width), jnp.float32)
                    for i in range(k + 1):
                        residual = residual + tiled(coef[i], 16, width) * y[i, chunk, span].astype(jnp.float32)
                        residual = residual + tiled(coef[4 + i], 16, width) * x[i, chunk, span].astype(jnp.float32)
                    below = jnp.abs(diag[chunk, span] - ritz) + 1.0
                    x[k + 1, chunk, span] = (residual / below).astype(jnp.bfloat16)
                return carry

            lax.fori_loop(0, 2 * rb, correct, 0)

    ritz_rows = jnp.zeros((half, width), jnp.float32)
    image_rows = jnp.zeros((half, width), jnp.float32)
    for i in range(ITERS + 1):
        alpha = tiled(coef[i], half, width)
        ritz_rows = ritz_rows + alpha * x[i, mine].astype(jnp.float32)
        image_rows = image_rows + alpha * y_own[i]
    ritz_ref[wi] = ritz_rows
    residual_ref[wi] = image_rows - tiled(coef[8], half, width) * ritz_rows
    copies = [
        pltpu.make_async_remote_copy(
            src_ref=ref.at[wi], dst_ref=ref.at[wi], send_sem=out_send.at[n], recv_sem=out_recv.at[n],
            device_id={"wa": other}, device_id_type=MESH,
        )
        for n, ref in enumerate((ritz_ref, residual_ref))
    ]
    for copy in copies:
        copy.start()
    wait_bytes(sc_xy.at[0, pl.ds(0, rb - 1)], xy_send.at[0])
    for k in range(1, ITERS + 1):
        wait_bytes(sc_xy.at[k, pl.ds(0, rb - 1)], xy_send.at[k])
    for k in range(ITERS + 1):
        wait_bytes(sc_z.at[k, pl.ds(0, 2 * lb - 1)], z_send.at[k])
    for copy in copies:
        copy.wait()


def dense_operator(operator_blocks, operator_pairs, levels):
    symmetric = 0.5 * (operator_blocks + jnp.swapaxes(operator_blocks, 1, 2))
    indices = jnp.arange(levels, dtype=jnp.int32)
    left_hot = (operator_pairs[:, 0:1] == indices[None, :]).astype(jnp.float32)
    right_hot = (operator_pairs[:, 1:2] == indices[None, :]).astype(jnp.float32)
    return jnp.einsum("nw,nv,nts->wvts", left_hot, right_hot, symmetric, precision=highest)


def per_device(initial_guess, left_environment, right_environment, operator_blocks, operator_pairs):
    own, physical, window = initial_guess.shape
    width = physical * window
    levels = right_environment.shape[1]
    local_levels, lb, _, _, depth = left_environment.shape
    rb, wa = lax.axis_size("rb"), lax.axis_size("wa")
    half = own // wa
    side = 1
    while side * side < rb:
        side += 1
    level_index = lax.axis_index("wa")

    operator = dense_operator(operator_blocks, operator_pairs, levels)
    local_operator = lax.dynamic_slice_in_dim(operator, level_index * local_levels, local_levels, 0)
    joint = jnp.einsum(
        "kvts,cvb->ksctb", local_operator, right_environment.astype(jnp.float32), precision=highest
    )
    joint = joint.reshape(local_levels * width, width).astype(jnp.bfloat16)
    operator_diag = jnp.diagonal(operator, axis1=2, axis2=3)
    right_diag = jnp.diagonal(right_environment, axis1=0, axis2=2).astype(jnp.float32)
    level_rows = jnp.einsum("kvs,vb->ksb", operator_diag, right_diag, precision=highest)
    level_rows = jnp.pad(level_rows.reshape(levels, width), ((0, 128 - levels), (0, 0)))

    guess = initial_guess.reshape(wa, half, width)
    left = left_environment.reshape(local_levels, lb, own, depth)
    sizes = (lb, rb, wa, side, half, width, levels, own * lb * rb * width)
    f32, bf16 = jnp.float32, jnp.bfloat16
    DMA = pltpu.SemaphoreType.DMA
    n = ITERS + 1
    vmem = pl.BlockSpec(memory_space=pltpu.VMEM)
    ritz, residual = pl.pallas_call(
        functools.partial(davidson_kernel, sizes),
        out_shape=[jax.ShapeDtypeStruct((wa, half, width), f32)] * 2,
        in_specs=[vmem, pl.BlockSpec(memory_space=pl.ANY), vmem, vmem],
        out_specs=[vmem, vmem],
        scratch_shapes=[
            pltpu.VMEM((local_levels, lb, own, depth), bf16),
            pltpu.VMEM((n, 2 * rb, half, width), bf16),
            pltpu.VMEM((ITERS, 2 * rb, half, width), bf16),
            pltpu.VMEM((n, half, width), f32),
            pltpu.VMEM((lb * own, local_levels * width), bf16),
            pltpu.VMEM((lb, 2, half, width), f32),
            pltpu.VMEM((lb, half, width), bf16),
            pltpu.VMEM((lb, half, width), bf16),
            pltpu.VMEM((lb, half, width), bf16),
            pltpu.VMEM((lb, half, width), bf16),
            pltpu.VMEM((own, 128), bf16),
            pltpu.VMEM((own, 128), bf16),
            pltpu.VMEM((2 * rb, half, 128), bf16),
            pltpu.VMEM((2 * rb, half, width), f32),
            pltpu.VMEM((9,) + TILE, f32),
            pltpu.VMEM((n, rb) + TILE, f32),
            pltpu.VMEM((n, 2 * lb) + TILE, f32),
            DMA((lb,)),
            DMA((2 + ITERS,)),
            DMA((2 + ITERS, rb)),
            DMA((2 + ITERS,)),
            DMA((2 + ITERS,)),
            DMA((n,)),
            DMA((n,)),
            DMA((n,)),
            DMA((n,)),
            DMA((n, 2)),
            DMA((n, 2)),
            DMA((n,)),
            DMA((n,)),
            DMA((3,)),
            DMA((3,)),
        ],
        compiler_params=pltpu.CompilerParams(
            collective_id=0, has_side_effects=True, vmem_limit_bytes=60 * 1024 * 1024
        ),
    )(guess, left, joint, level_rows)
    return ritz.reshape(own, physical, window), residual.reshape(own, physical, window)


def solution(mesh):
    in_specs = (P(("lb", "rb"), None, None), P("wa", None, "rb", None, "lb"), P(), P(), P())
    out_specs = (P(("lb", "rb"), None, None), P(("lb", "rb"), None, None))
    return jax.shard_map(
        per_device, mesh=mesh, in_specs=in_specs, out_specs=out_specs, check_vma=False
    )
```

profile of v0, /device:TPU:1, one launch (start us, length us, event | category | flops | bytes accessed | tf_op | source)
XLA Modules:
  0.0 153.5 jit_solution(13739676817916482630)
XLA Ops:
  0.6 0.8 slice_bitcast_fusion.1
  1.4 1.4 fusion.1
  2.8 0.1 dynamic-slice_bitcast_fusion
  2.9 0.2 copy.20
  3.1 3.6 %convert_bitcast_fusion = bf16[4,4,128,4,128]{4,1,2,3,0:T(4,128)(2,1)S(1)} fusion(f32[4,8,4,4,1]{1,3,4,2,0:T(4,128)S(1)} %copy.20, bf16[128,8,128]{2,1,0:T(8,128)(2,1)} %param.7), kind=kOutput, calls=%fused_computation.3 | convolution fusion | flops 101711872 | bytes 2361344 | tf_op jit(solution)/shard_map/kvts,cvb->ksctb/dot_general | solution.py:415
  6.8 0.0 copy-start
  6.8 1.6 %copy.15 = bf16[4,4,128,4,128]{4,3,2,1,0:T(4,128)(2,1)S(1)} copy(bf16[4,4,128,4,128]{4,1,2,3,0:T(4,128)(2,1)S(1)} %convert_bitcast_fusion) | data formatting | bytes 4194304 | tf_op jit(solution)/shard_map/convert_element_type | solution.py:418
  8.4 0.0 copy-start.1
  8.4 1.7 %copy.32 = bf16[256,8,4,128]{3,1,2,0:T(8,128)(2,1)} copy(bf16[256,8,4,128]{3,2,1,0:T(4,128)(2,1)S(1)} %bitcast.52) | data formatting | bytes 4194304
  10.1 0.1 copy.16
  10.2 0.6 gather_fusion
  10.8 0.0 copy-done
  10.8 3.4 %copy.17 = bf16[128,8,128]{1,2,0:T(8,128)(2,1)} copy(bf16[128,8,128]{2,1,0:T(8,128)(2,1)S(1)} %copy-done) | data formatting | bytes 524288 | tf_op args[2]
  14.2 1.9 %gather_fusion.1 = bf16[128,8]{1,0:T(8,128)(2,1)S(1)} fusion(bf16[8,128,128]{0,2,1:T(8,128)(2,1)} %bitcast.53, s32[128]{0:T(128)S(1)} %or_bitcast_fusion), kind=kCustom, calls=%fused_computation.1 | custom fusion | bytes 5120 | tf_op jit(solution)/shard_map/jit(diagonal)/gather | solution.py:420
  16.1 0.1 convolution_bitcast_fusion
  16.2 0.8 pad.4.level_ref
  17.0 0.0 copy-done.1
  17.0 0.7 reshape.21.guess_ref
  17.7 132.6 %shard_map.68 = (f32[2,32,512]{2,1,0:T(8,128)}, f32[2,32,512]{2,1,0:T(8,128)}) custom-call(bf16[2,32,512]{2,1,0:T(8,128)(2,1)} %reshape.21.guess_ref, bf16[4,8,64,1024]{3,2,1,0:T(8,128)(2,1)} %bitcast.54, bf16[2048,512]{1,0:T(8,128)(2,1)} %bitcast.51, f32[128,512]{1,0:T(8,128)} %pad.4.level_ref), custom_call_target="tpu_custom_call" | custom-call | tf_op jit(solution)/shard_map/pallas_call | solution.py:431
  150.3 1.6 %reshape.24 = f32[64,4,128]{2,1,0:T(4,128)} reshape(f32[2,32,512]{2,1,0:T(8,128)} %get-tuple-element.4) | data formatting | bytes 262144 | tf_op jit(solution)/shard_map/reshape | solution.py:474
  151.9 1.6 %reshape.25 = f32[64,4,128]{2,1,0:T(4,128)} reshape(f32[2,32,512]{2,1,0:T(8,128)} %get-tuple-element.5) | data formatting | bytes 262144 | tf_op jit(solution)/shard_map/reshape | solution.py:474
  (3 shorter events, 0.0 us)
Async XLA Ops:
  6.8 4.0 %copy-start = (bf16[128,8,128]{2,1,0:T(8,128)(2,1)S(1)}, bf16[128,8,128]{2,1,0:T(8,128)(2,1)}, u32[]{:S(2)}) copy-start(bf16[128,8,128]{2,1,0:T(8,128)(2,1)} %param.7) | copy-start | bytes 786436
  8.4 8.6 %copy-start.1 = (bf16[64,4,128]{2,1,0:T(4,128)(2,1)S(1)}, bf16[64,4,128]{2,1,0:T(4,128)(2,1)}, u32[]{:S(2)}) copy-start(bf16[64,4,128]{2,1,0:T(4,128)(2,1)} %param.5) | copy-start | bytes 196612
where the time goes:
time: 154 us
  Pallas kernels  133 us (86%)
  local copies, waits for them, and re-layouts  15 us (10%)
  matrix products  5.18 us (3%)
    pallas_call x1, Pallas kernels, per_device(): pl.pallas_call(functools.partial(davidson_kernel, sizes), out_shape=[jax....  133 us
    unnamed x6, local copies, waits for them, and re-layouts  5.08 us
    dot_general x1, matrix products, per_device(): jnp.einsum('kvts,cvb->ksctb', local_operator, right_environment.astype(jn...  3.64 us

commit v1 on v0

v1 whole, which is shorter than its diff:
```python
import functools

import jax
import jax.numpy as jnp
from jax import lax
from jax.experimental import pallas as pl
from jax.experimental.pallas import tpu as pltpu
from jax.sharding import PartitionSpec as P

ITERS = 3
SWEEPS = 8

epsilon = 1e-06

TILE = (8, 128)
MESH = pl.DeviceIdType.MESH

FAR = (4, 3, -3)
NEAR = (2, -2, 1, -1, 0)


def half_angle(y, x):
    square = x * x + y * y
    zero = square == 0.0
    inverse = lax.rsqrt(jnp.where(zero, 1.0, square))
    half = 0.5 + 0.5 * (jnp.abs(x) * inverse)
    root = lax.rsqrt(half)
    big = half * root
    small = 0.5 * (jnp.abs(y) * inverse) * root
    positive = x >= 0.0
    cosine = jnp.where(positive, big, small)
    sine = jnp.where(positive, small, big)
    sine = jnp.where(y < 0.0, -sine, sine)
    return jnp.where(zero, 1.0, cosine), jnp.where(zero, 0.0, sine)


def lowest(entries, order):
    one, none = jnp.full(TILE, 1.0, jnp.float32), jnp.full(TILE, 0.0, jnp.float32)
    if order == 1:
        return entries[(0, 0)], [one]

    def at(i, j):
        return (min(i, j), max(i, j))

    keys = [(i, j) for i in range(order) for j in range(i, order)]
    largest = functools.reduce(jnp.maximum, [jnp.abs(entries[key]) for key in keys])
    unit = jnp.where(largest == 0.0, 1.0, largest)
    start = tuple((entries[key] / unit) * 2.0**59 for key in keys)
    vectors0 = tuple(one if i == j else none for i in range(order) for j in range(order))

    def sweep(_, carry):
        m = dict(zip(keys, carry[0]))
        v = list(carry[1])
        for p in range(order):
            for q in range(p + 1, order):
                a, b, d = m[(p, p)], m[(p, q)], m[(q, q)]
                c, s = half_angle(2.0 * b, d - a)
                m[(p, p)] = c * (c * a - s * b) - s * (c * b - s * d)
                m[(p, q)] = s * (c * a - s * b) + c * (c * b - s * d)
                m[(q, q)] = s * (s * a + c * b) + c * (s * b + c * d)
                for i in range(order):
                    if i != p and i != q:
                        x, y = m[at(i, p)], m[at(i, q)]
                        m[at(i, p)] = c * x - s * y
                        m[at(i, q)] = s * x + c * y
                    x, y = v[i * order + p], v[i * order + q]
                    v[i * order + p] = c * x - s * y
                    v[i * order + q] = s * x + c * y
        return tuple(m[key] for key in keys), tuple(v)

    values, vectors = lax.fori_loop(0, SWEEPS, sweep, (start, vectors0))
    m = dict(zip(keys, values))
    best = m[(0, 0)]
    weights = [vectors[i * order] for i in range(order)]
    for j in range(1, order):
        better = m[(j, j)] < best
        best = jnp.where(better, m[(j, j)], best)
        weights = [jnp.where(better, vectors[i * order + j], weights[i]) for i in range(order)]
    sign = jnp.where(weights[0] < 0.0, -1.0, 1.0)
    return best * 2.0**-59 * unit, [weight * sign for weight in weights]


def tiled(value, rows, columns):
    wide = jnp.concatenate([value] * (columns // 128), axis=1)
    return jnp.concatenate([wide] * (rows // 8), axis=0)


def wait_bytes(ref, sem):
    pltpu.make_async_copy(ref, ref, sem).wait()


def davidson_kernel(sizes, guess_ref, left_hbm, right_ref, blocks_ref, pairs_ref, ritz_ref, residual_ref,
                    joint_ref, level_ref, right_whole, right32, right_rows, symmetric, guess_rows, lv_far, lv_near, x, y, y_own,
                    z_far, z_near, part_far, part_near, far_out, far_in, near_out, near_in,
                    relay_out, relay_in, relay4_in, rs_out, rs_in,
                    dl_mine, dl_swap, dl_all, diag, coef, sc_xy, sc_z,
                    left_sem, gather_send, gather_recv, fwd_send, fwd_recv, column_send, column_recv,
                    xy_send, xy_recv, z_send, z_recv, swap_send, swap_recv,
                    relay_send, relay_recv, relay4_recv, rs_send, rs_recv, out_send, out_recv):
    lb, rb, wa, side, half, width, window, levels, total_count = sizes
    own = 2 * half
    li, ri, wi = lax.axis_index("lb"), lax.axis_index("rb"), lax.axis_index("wa")
    other = 1 - wi
    xi, yi = lax.div(ri, side), lax.rem(ri, side)
    mine = ri * 2 + wi
    chunks = 2 * rb
    own_column = chunks + li
    xs = [lax.rem(xi + step, side) for step in range(side)]
    ys = [lax.rem(yi + step, side) for step in range(side)]
    zs = [lax.rem(li + step, lb) for step in range(lb)]
    plane_steps = sorted(
        range(1, rb),
        key=lambda step: -min(step // side, side - step // side) - min(step % side, side - step % side),
    )
    column_steps = sorted(range(1, lb), key=lambda step: -min(step, lb - step))

    def plane_peer(step):
        return xs[step // side] * side + ys[step % side]

    def plane_source(step):
        return xs[-(step // side) % side] * side + ys[-(step % side) % side]

    for steps, held, first in ((FAR, lv_far, 0), (NEAR, lv_near, len(FAR))):
        for place, step in enumerate(steps):
            pltpu.make_async_copy(
                left_hbm.at[:, (li + step + lb) % lb], held.at[:, place], left_sem.at[first + place]
            ).start()

    barrier = pltpu.get_barrier_semaphore()

    for step in plane_steps:
        pl.semaphore_signal(barrier, inc=1, device_id={"rb": plane_peer(step)}, device_id_type=MESH)
    for step in range(lb):
        for turn in range(2):
            if step or turn:
                pl.semaphore_signal(
                    barrier, inc=1,
                    device_id={"lb": zs[step], "wa": other if turn else wi}, device_id_type=MESH,
                )

    def gather_start(number, source, buf):
        for step in plane_steps:
            pltpu.make_async_remote_copy(
                src_ref=source, dst_ref=buf.at[mine],
                send_sem=gather_send.at[number], recv_sem=gather_recv.at[number, step],
                device_id={"rb": plane_peer(step)}, device_id_type=MESH,
            ).start()
        for step in column_steps:
            pltpu.make_async_remote_copy(
                src_ref=source, dst_ref=buf.at[own_column],
                send_sem=column_send.at[number], recv_sem=column_recv.at[number],
                device_id={"lb": zs[step]}, device_id_type=MESH,
            ).start()

    def forward(number, source, buf, slot):
        pltpu.make_async_remote_copy(
            src_ref=source, dst_ref=buf.at[slot],
            send_sem=fwd_send.at[number], recv_sem=fwd_recv.at[number],
            device_id={"wa": other}, device_id_type=MESH,
        ).start()

    def gather_forward(number, buf, steps):
        for step in steps:
            slot = plane_source(step) * 2 + wi
            wait_bytes(buf.at[slot], gather_recv.at[number, step])
            forward(number, buf.at[slot], buf, slot)

    def gather_finish(number, buf, count):
        wait_bytes(buf.at[pl.ds(0, count)], fwd_recv.at[number])
        wait_bytes(buf.at[pl.ds(0, lb - 1)], column_recv.at[number])

    def gather_drain(number, buf, count):
        wait_bytes(buf.at[pl.ds(0, count)], fwd_send.at[number])
        wait_bytes(buf.at[pl.ds(0, lb - 1)], column_send.at[number])
        wait_bytes(buf.at[pl.ds(0, rb - 1)], gather_send.at[number])

    own_guess = guess_ref[...].astype(jnp.float32)
    right_whole[...] = right_ref[...].astype(jnp.float32)
    for v in range(levels):
        right32[v] = right_whole[:, v, :]
    physical = width // window
    guess_rows[...] = own_guess
    for s in range(physical):
        piece = guess_rows[:, s, :].astype(jnp.bfloat16)
        for h in range(2):
            x[0, ri * 2 + h, :, s * window : (s + 1) * window] = piece[h * half : (h + 1) * half]
    x[0, own_column] = x[0, mine]

    count = blocks_ref.shape[2]
    states = [(t, s) for t in range(physical) for s in range(t, physical)]

    def symmetrize(n, carry):
        for place, (t, s) in enumerate(states):
            symmetric[n, place] = 0.5 * (blocks_ref[t, s, n] + blocks_ref[s, t, n])
        return carry

    lax.fori_loop(0, count, symmetrize, 0)
    chunk_rows = 32

    def joint_body(index, carry):
        level, chunk = index // (window // chunk_rows), index % (window // chunk_rows)
        start = pl.multiple_of(chunk * chunk_rows, chunk_rows)

        def add_block(n, sums):
            here = jnp.where(pairs_ref[0, n] == wi * (levels // 2) + level, 1.0, 0.0)
            slab = right32[pairs_ref[1, n], pl.ds(start, chunk_rows)] * here
            return tuple(total + symmetric[n, place] * slab for place, total in enumerate(sums))

        sums = lax.fori_loop(
            0, count, add_block,
            tuple(jnp.zeros((chunk_rows, window), jnp.float32) for _ in states),
        )
        for place, (t, s) in enumerate(states):
            block = sums[place].astype(jnp.bfloat16)
            for a, b in {(t, s), (s, t)}:
                joint_ref[
                    pl.ds(pl.multiple_of(level * width + a * window + start, chunk_rows), chunk_rows),
                    b * window : (b + 1) * window,
                ] = block
        return carry

    joint_steps = (levels // 2) * (window // chunk_rows)
    lax.fori_loop(0, joint_steps // 2, joint_body, 0)
    pl.semaphore_wait(barrier, rb - 1 + 2 * lb - 1)
    gather_start(0, x.at[0, mine], x.at[0])
    lax.fori_loop(joint_steps // 2, joint_steps, joint_body, 0)

    eye = lax.broadcasted_iota(jnp.int32, (window, window), 0) == lax.broadcasted_iota(
        jnp.int32, (window, window), 1
    )
    for v in range(levels):
        right_rows[v : v + 1] = jnp.sum(jnp.where(eye, right32[v], 0.0), axis=0, keepdims=True)
    level_row = lax.broadcasted_iota(jnp.int32, (levels, window), 0)

    def add_level(n, sums):
        hit = jnp.where(level_row == pairs_ref[0, n], right_rows[pl.ds(pairs_ref[1, n], 1)], 0.0)
        return tuple(total + blocks_ref[s, s, n] * hit for s, total in enumerate(sums))

    level_ref[...] = jnp.zeros_like(level_ref)
    level_ref[:levels] = jnp.concatenate(
        lax.fori_loop(0, count, add_level, tuple(jnp.zeros((levels, window), jnp.float32) for _ in range(physical))),
        axis=1,
    )

    for held, first in ((lv_far, 0), (lv_near, len(FAR))):
        for place in range(held.shape[1]):
            wait_bytes(held.at[:, place], left_sem.at[first + place])
    per_tile = 128 // own
    lane = lax.broadcasted_iota(jnp.int32, (own, 128), 1)
    row = lax.broadcasted_iota(jnp.int32, (own, 128), 0)
    hit = lane == row + (ri % per_tile) * own
    entries = jnp.zeros((own, 128), jnp.float32)
    for level in range(levels // 2):
        block = lv_near[level, NEAR.index(0), :, pl.ds(pl.multiple_of((ri // per_tile) * 128, 128), 128)]
        column = jnp.sum(jnp.where(hit, block.astype(jnp.float32), 0.0), axis=1, keepdims=True)
        entries = entries + jnp.where(lane == wi * (levels // 2) + level, column, 0.0)
    dl_mine[...] = entries.astype(jnp.bfloat16)
    swap_diag = pltpu.make_async_remote_copy(
        src_ref=dl_mine, dst_ref=dl_swap, send_sem=out_send.at[2], recv_sem=out_recv.at[2],
        device_id={"wa": other}, device_id_type=MESH,
    )
    swap_diag.start()
    gather_forward(0, x.at[0], plane_steps)
    swap_diag.wait()
    both = (dl_mine[...].astype(jnp.float32) + dl_swap[...].astype(jnp.float32)).astype(jnp.bfloat16)
    dl_all[ri * 2] = both[:half]
    dl_all[ri * 2 + 1] = both[half:]
    dl_all[own_column] = dl_all[mine]
    gather_start(1, dl_all.at[mine], dl_all)
    gather_finish(0, x.at[0], rb - 1)

    gram, cross, mix = {}, {}, {}
    for k in range(ITERS + 1):
        def left_product(held, into, first, count):
            rows = held.shape[1] * own
            product = jnp.dot(
                held[first : first + count].reshape(count * rows, lb_depth),
                x[k, :chunks].reshape(lb_depth, width),
                preferred_element_type=jnp.float32,
            ).astype(jnp.bfloat16)
            for n in range(count):
                into[:, (first + n) * width : (first + n + 1) * width] = product[n * rows : (n + 1) * rows]

        def joint_product(held, part, swap_out):
            places = part.shape[0]
            part[...] = jnp.dot(
                held[...], joint_ref[...], preferred_element_type=jnp.float32
            ).reshape(places, 2, half, width)
            for place in range(places):
                swap_out[place] = part[place, other].astype(jnp.bfloat16)

        def swap_copy(turn, swap_out, swap_in):
            return pltpu.make_async_remote_copy(
                src_ref=swap_out, dst_ref=swap_in,
                send_sem=swap_send.at[k, turn], recv_sem=swap_recv.at[k, turn],
                device_id={"wa": other}, device_id_type=MESH,
            )

        def along(source, target, send_sem, recv_sem, step):
            pltpu.make_async_remote_copy(
                src_ref=source, dst_ref=target, send_sem=send_sem, recv_sem=recv_sem,
                device_id={"lb": zs[step % lb]}, device_id_type=MESH,
            ).start()

        def products(first, second):
            return jnp.sum((first * second).reshape(half // 8, 8, width), axis=0)

        def folded(sums):
            line = jnp.sum(sums, axis=0, keepdims=True)
            short = line[:, :128]
            for column in range(1, width // 128):
                short = short + line[:, column * 128 : (column + 1) * 128]
            return short

        def add_cross(sums, total, step):
            return [
                done + products(x[j, chunks + zs[step % lb]].astype(jnp.float32), total)
                for j, done in enumerate(sums)
            ]

        lb_depth = rb * own
        held_levels = levels // 2
        left_product(lv_far, z_far, 0, held_levels)
        joint_product(z_far, part_far, far_out)
        far_swap = swap_copy(0, far_out, far_in)
        far_swap.start()
        left_product(lv_near, z_near, 0, held_levels // 2)
        far_swap.wait()
        for place in range(len(FAR)):
            total = part_far[place, wi] + far_in[place].astype(jnp.float32)
            relay_out[place] = total.astype(jnp.bfloat16)
        along(relay_out.at[0, :16], relay4_in.at[0], relay_send.at[k], relay4_recv.at[k], 2)
        along(relay_out.at[0, 16:], relay4_in.at[1], relay_send.at[k], relay4_recv.at[k], lb - 2)
        along(relay_out.at[1], relay_in.at[0], relay_send.at[k], relay_recv.at[k], 1)
        along(relay_out.at[2], relay_in.at[1], relay_send.at[k], relay_recv.at[k], lb - 1)
        cross_sums = [jnp.zeros((8, width), jnp.float32)] * (k + 1)
        for place, step in enumerate(FAR):
            total = part_far[place, wi] + far_in[place].astype(jnp.float32)
            cross_sums = add_cross(cross_sums, total, step)
        vector = x[k, mine].astype(jnp.float32)
        lines = [folded(products(x[j, mine].astype(jnp.float32), vector)) for j in range(k + 1)]
        left_product(lv_near, z_near, held_levels // 2, held_levels - held_levels // 2)
        joint_product(z_near, part_near, near_out)
        near_swap = swap_copy(1, near_out, near_in)
        near_swap.start()
        if k == 0:
            gather_forward(1, dl_all, plane_steps)
        near_swap.wait()
        for place in range(2, 4):
            total = part_near[place, wi] + near_in[place].astype(jnp.float32)
            rs_out[place] = total.astype(jnp.bfloat16)
            along(rs_out.at[place], rs_in.at[place], rs_send.at[k], rs_recv.at[k], NEAR[place])
        for place, step in enumerate(NEAR):
            total = part_near[place, wi] + near_in[place].astype(jnp.float32)
            cross_sums = add_cross(cross_sums, total, step)
        lines += [folded(sums) for sums in cross_sums]
        lines += [jnp.zeros((1, 128), jnp.float32)] * (8 - len(lines))
        sc_xy[k, ri] = jnp.concatenate(lines, axis=0)
        for step in plane_steps:
            pltpu.make_async_remote_copy(
                src_ref=sc_xy.at[k, ri], dst_ref=sc_xy.at[k, ri],
                send_sem=xy_send.at[k], recv_sem=xy_recv.at[k],
                device_id={"rb": plane_peer(step)}, device_id_type=MESH,
            ).start()
        wait_bytes(relay_in, relay_recv.at[k])
        wait_bytes(relay4_in, relay4_recv.at[k])
        for place in range(2):
            total = part_near[place, wi] + near_in[place].astype(jnp.float32)
            total = total + relay_in[place].astype(jnp.float32)
            extra = relay4_in[place].astype(jnp.float32)
            total = jnp.concatenate(
                [total[:16] + extra, total[16:]] if place == 0 else [total[:16], total[16:] + extra], axis=0
            )
            rs_out[place] = total.astype(jnp.bfloat16)
            along(rs_out.at[place], rs_in.at[place], rs_send.at[k], rs_recv.at[k], NEAR[place])

        def share_sums():
            wait_bytes(sc_xy.at[k, pl.ds(0, rb - 1)], xy_recv.at[k])
            summed = sc_xy[k, 0]
            for j in range(1, rb):
                summed = summed + sc_xy[k, j]
            sc_z[k, column_mine] = summed
            for step in range(lb):
                for turn in range(2):
                    if step or turn:
                        pltpu.make_async_remote_copy(
                            src_ref=sc_z.at[k, column_mine], dst_ref=sc_z.at[k, column_mine],
                            send_sem=z_send.at[k], recv_sem=z_recv.at[k],
                            device_id={"lb": zs[step], "wa": other if turn else wi},
                            device_id_type=MESH,
                        ).start()

        column_mine = li * 2 + wi
        if k == ITERS:
            share_sums()
        image = part_near[4, wi] + near_in[4].astype(jnp.float32)
        wait_bytes(rs_in, rs_recv.at[k])
        for place in range(4):
            image = image + rs_in[place].astype(jnp.float32)
        y_own[k] = image
        if k < ITERS:
            rounded = image.astype(jnp.bfloat16)
            y[k, mine] = rounded
            y[k, own_column] = rounded
            gather_start(2 + k, y.at[k, mine], y.at[k])
            forward(2 + k, y.at[k, mine], y.at[k], mine)
            share_sums()
        wait_bytes(rs_out, rs_send.at[k])
        wait_bytes(relay_out, relay_send.at[k])
        if k == 0:
            gather_finish(1, dl_all, rb - 1)
            rest = level_ref[...]
            found = jnp.zeros(((chunks + lb) * half, width), jnp.float32)
            for _ in range(3):
                term = rest.astype(jnp.bfloat16)
                rest = rest - term.astype(jnp.float32)
                found = found + jnp.dot(
                    dl_all[...].reshape((chunks + lb) * half, 128), term, preferred_element_type=jnp.float32
                )
            diag[...] = found.reshape(chunks + lb, half, width)
        early = len(plane_steps) // 2
        if k < ITERS:
            gather_forward(2 + k, y.at[k], plane_steps[:early])
        wait_bytes(sc_z.at[k, pl.ds(0, 2 * lb - 1)], z_recv.at[k])
        total = sc_z[k, 0]
        for j in range(1, 2 * lb):
            total = total + sc_z[k, j]
        total = jnp.sum(total, axis=1, keepdims=True) * (1.0 / total_count)
        scalars = [jnp.broadcast_to(total[q : q + 1], TILE) for q in range(2 * k + 2)]
        for j in range(k + 1):
            gram[(j, k)] = gram[(k, j)] = scalars[j]
            cross[(j, k)] = cross[(k, j)] = scalars[k + 1 + j]
        raw = [jnp.zeros(TILE, jnp.float32) for _ in range(k)] + [jnp.ones(TILE, jnp.float32)]
        for j in range(k):
            correlation = sum(mix[(j, i)] * gram[(i, k)] for i in range(j + 1))
            for i in range(j + 1):
                raw[i] = raw[i] - correlation * mix[(j, i)]
        norm = jnp.zeros(TILE, jnp.float32)
        for i in range(k + 1):
            norm = norm + raw[i] * sum(raw[j] * gram[(i, j)] for j in range(k + 1))
        scale = lax.rsqrt(jnp.maximum(norm, 0.0) + epsilon)
        for i in range(k + 1):
            mix[(k, i)] = raw[i] * scale
        entries = {}
        for b in range(k + 1):
            image_row = [
                sum(mix[(b, j)] * cross[(i, j)] for j in range(b + 1)) for i in range(b + 1)
            ]
            for a in range(b + 1):
                entries[(a, b)] = sum(mix[(a, i)] * image_row[i] for i in range(a + 1))
        theta, weights = lowest(entries, k + 1)
        alphas = [
            sum(weights[j] * mix[(j, i)] for j in range(i, k + 1)) for i in range(k + 1)
        ]
        for i in range(k + 1):
            coef[i] = alphas[i]
            coef[4 + i] = -(theta * alphas[i])
        coef[8] = theta

        if k < ITERS:
            gather_forward(2 + k, y.at[k], plane_steps[early:])
            gather_finish(2 + k, y.at[k], rb)

            def correct(chunk, carry):
                for start in range(0, half, 16):
                    span = pl.ds(start, 16)
                    ritz = tiled(coef[8], 16, width)
                    residual = jnp.zeros((16, width), jnp.float32)
                    for i in range(k + 1):
                        residual = residual + tiled(coef[i], 16, width) * y[i, chunk, span].astype(jnp.float32)
                        residual = residual + tiled(coef[4 + i], 16, width) * x[i, chunk, span].astype(jnp.float32)
                    below = jnp.abs(diag[chunk, span] - ritz) + 1.0
                    x[k + 1, chunk, span] = (residual / below).astype(jnp.bfloat16)
                return carry

            lax.fori_loop(0, chunks + lb, correct, 0)

    ritz_rows = jnp.zeros((half, width), jnp.float32)
    image_rows = jnp.zeros((half, width), jnp.float32)
    for i in range(ITERS + 1):
        alpha = tiled(coef[i], half, width)
        ritz_rows = ritz_rows + alpha * x[i, mine].astype(jnp.float32)
        image_rows = image_rows + alpha * y_own[i]
    image_rows = image_rows - tiled(coef[8], half, width) * ritz_rows
    my_rows = pl.ds(pl.multiple_of(wi * half, half), half)
    copies = []
    for n, (ref, rows) in enumerate(((ritz_ref, ritz_rows), (residual_ref, image_rows))):
        for s in range(physical):
            ref[my_rows, s, :] = rows[:, s * window : (s + 1) * window]
        copies.append(
            pltpu.make_async_remote_copy(
                src_ref=ref.at[my_rows], dst_ref=ref.at[my_rows],
                send_sem=out_send.at[n], recv_sem=out_recv.at[n],
                device_id={"wa": other}, device_id_type=MESH,
            )
        )
    for copy in copies:
        copy.start()
    gather_drain(0, x.at[0], rb - 1)
    gather_drain(1, dl_all, rb - 1)
    for k in range(ITERS):
        gather_drain(2 + k, y.at[k], rb)
    wait_bytes(sc_xy.at[0, pl.ds(0, rb - 1)], xy_send.at[0])
    for k in range(1, ITERS + 1):
        wait_bytes(sc_xy.at[k, pl.ds(0, rb - 1)], xy_send.at[k])
    for k in range(ITERS + 1):
        wait_bytes(sc_z.at[k, pl.ds(0, 2 * lb - 1)], z_send.at[k])
    for copy in copies:
        copy.wait()


def per_device(initial_guess, left_environment, right_environment, operator_blocks, operator_pairs):
    own, physical, window = initial_guess.shape
    width = physical * window
    levels = right_environment.shape[1]
    local_levels, lb, _, _, depth = left_environment.shape
    rb, wa = lax.axis_size("rb"), lax.axis_size("wa")
    half = own // wa
    side = 1
    while side * side < rb:
        side += 1
    left = left_environment.reshape(local_levels, lb, own, depth)
    sizes = (lb, rb, wa, side, half, width, window, levels, own * lb * rb * width)
    f32, bf16 = jnp.float32, jnp.bfloat16
    DMA = pltpu.SemaphoreType.DMA
    n = ITERS + 1
    vmem = pl.BlockSpec(memory_space=pltpu.VMEM)
    smem = pl.BlockSpec(memory_space=pltpu.SMEM)
    blocks = operator_blocks.shape[0]
    pairs_of_states = physical * (physical + 1) // 2
    ritz, residual = pl.pallas_call(
        functools.partial(davidson_kernel, sizes),
        out_shape=[jax.ShapeDtypeStruct((own, physical, window), f32)] * 2,
        in_specs=[vmem, pl.BlockSpec(memory_space=pl.ANY), vmem, smem, smem],
        out_specs=[vmem, vmem],
        scratch_shapes=[
            pltpu.VMEM((local_levels * width, width), bf16),
            pltpu.VMEM((128, width), f32),
            pltpu.VMEM((window, levels, window), f32),
            pltpu.VMEM((levels, window, window), f32),
            pltpu.VMEM((levels, window), f32),
            pltpu.SMEM((blocks, pairs_of_states), f32),
            pltpu.VMEM((own, physical, window), f32),
            pltpu.VMEM((local_levels, len(FAR), own, depth), bf16),
            pltpu.VMEM((local_levels, len(NEAR), own, depth), bf16),
            pltpu.VMEM((n, 2 * rb + lb, half, width), bf16),
            pltpu.VMEM((ITERS, 2 * rb + lb, half, width), bf16),
            pltpu.VMEM((n, half, width), f32),
            pltpu.VMEM((len(FAR) * own, local_levels * width), bf16),
            pltpu.VMEM((len(NEAR) * own, local_levels * width), bf16),
            pltpu.VMEM((len(FAR), 2, half, width), f32),
            pltpu.VMEM((len(NEAR), 2, half, width), f32),
            pltpu.VMEM((len(FAR), half, width), bf16),
            pltpu.VMEM((len(FAR), half, width), bf16),
            pltpu.VMEM((len(NEAR), half, width), bf16),
            pltpu.VMEM((len(NEAR), half, width), bf16),
            pltpu.VMEM((len(FAR), half, width), bf16),
            pltpu.VMEM((2, half, width), bf16),
            pltpu.VMEM((2, half // 2, width), bf16),
            pltpu.VMEM((4, half, width), bf16),
            pltpu.VMEM((4, half, width), bf16),
            pltpu.VMEM((own, 128), bf16),
            pltpu.VMEM((own, 128), bf16),
            pltpu.VMEM((2 * rb + lb, half, 128), bf16),
            pltpu.VMEM((2 * rb + lb, half, width), f32),
            pltpu.VMEM((9,) + TILE, f32),
            pltpu.VMEM((n, rb) + TILE, f32),
            pltpu.VMEM((n, 2 * lb) + TILE, f32),
            DMA((lb,)),
            DMA((2 + ITERS,)),
            DMA((2 + ITERS, rb)),
            DMA((2 + ITERS,)),
            DMA((2 + ITERS,)),
            DMA((2 + ITERS,)),
            DMA((2 + ITERS,)),
            DMA((n,)),
            DMA((n,)),
            DMA((n,)),
            DMA((n,)),
            DMA((n, 2)),
            DMA((n, 2)),
            DMA((n,)),
            DMA((n,)),
            DMA((n,)),
            DMA((n,)),
            DMA((n,)),
            DMA((3,)),
            DMA((3,)),
        ],
        compiler_params=pltpu.CompilerParams(
            collective_id=0, has_side_effects=True, vmem_limit_bytes=60 * 1024 * 1024
        ),
    )(
        initial_guess, left, right_environment,
        jnp.transpose(operator_blocks, (1, 2, 0)), jnp.transpose(operator_pairs),
    )
    return ritz, residual


def solution(mesh):
    in_specs = (P(("lb", "rb"), None, None), P("wa", None, "rb", None, "lb"), P(), P(), P())
    out_specs = (P(("lb", "rb"), None, None), P(("lb", "rb"), None, None))
    return jax.shard_map(
        per_device, mesh=mesh, in_specs=in_specs, out_specs=out_specs, check_vma=False
    )
```

time: 154 us -> 118 us (0.77)
  Pallas kernels: 133 us -> 114 us
  local copies, waits for them, and re-layouts: 15 us -> 3.14 us
  matrix products: 5.18 us -> 0 us
    pallas_call x1, Pallas kernels: 133 us -> 114 us  [per_device(): pl.pallas_call(functools.partial(davidson_kernel, sizes), out_shape=[jax....]
    dot_general x3 -> x0, matrix products: 5.18 us -> none  [the longest x1 3.64 us: per_device(): jnp.einsum('kvts,cvb->ksctb', local_operator, right_environment.astype(jn...]
    reshape x3 -> x0, local copies, waits for them, and re-layouts: 3.86 us -> none  [the longest x1 1.6 us: per_device(): ritz.reshape(own, physical, window)]
    gather x2 -> x0, local copies, waits for them, and re-layouts: 2.5 us -> none  [the longest x1 1.95 us: per_device(): jnp.diagonal(right_environment, axis1=0, axis2=2).astype(jnp.float32)]
    unnamed x6 -> x2, local copies, waits for them, and re-layouts: 5.08 us -> 3.14 us
    convert_element_type x1 -> x0, local copies, waits for them, and re-layouts: 1.62 us -> none  [per_device(): joint = joint.reshape(local_levels * width, width).astype(jnp.bfloat16)]
where the time goes in v1:
time: 118 us
  Pallas kernels  114 us (97%)
  local copies, waits for them, and re-layouts  3.14 us (3%)
    pallas_call x1, Pallas kernels, per_device(): pl.pallas_call(functools.partial(davidson_kernel, sizes), out_shape=[jax....  114 us
    unnamed x2, local copies, waits for them, and re-layouts  3.14 us

profile of v1, /device:TPU:1, one launch (start us, length us, event | category | flops | bytes accessed | tf_op | source)
XLA Modules:
  0.0 118.1 jit_solution(16436520468647818662)
XLA Ops:
  0.6 114.3 %shard_map.68 = (f32[64,4,128]{2,1,0:T(4,128)}, f32[64,4,128]{2,1,0:T(4,128)}) custom-call(bf16[64,4,128]{2,1,0:T(4,128)(2,1)} %guess_ref.1, bf16[4,8,64,1024]{3,2,1,0:T(8,128)(2,1)} %bitcast.3, bf16[128,8,128]{2,1,0:T(8,128)(2,1)} %right_ref.1, f32[4,4,16]{2,1,0:T(4,128)} %bitcast.4, s32[2,16]{1,0:T(2,128)} %bitcast.5), custom_call_target="tpu_custom_call" | custom-call | tf_op jit(solution)/shard_map/pallas_call | solution.py:531
  114.9 1.6 %copy.9 = f32[64,4,128]{2,1,0:T(4,128)} copy(f32[64,4,128]{2,1,0:T(4,128)} %get-tuple-element.4) | data formatting | bytes 262144
  116.5 1.6 %copy.10 = f32[64,4,128]{2,1,0:T(4,128)} copy(f32[64,4,128]{2,1,0:T(4,128)} %get-tuple-element.5) | data formatting | bytes 262144

commit v2 on v1

--- a/solution.py
+++ b/solution.py
@@ -96,7 +96,7 @@
                     dl_mine, dl_swap, dl_all, diag, coef, sc_xy, sc_z,
                     left_sem, gather_send, gather_recv, fwd_send, fwd_recv, column_send, column_recv,
                     xy_send, xy_recv, z_send, z_recv, swap_send, swap_recv,
-                    relay_send, relay_recv, relay4_recv, rs_send, rs_recv, out_send, out_recv):
+                    relay_send, relay_recv, relay4_recv, rs_send, rs_recv, own_send, own_recv, diag_sem):
     lb, rb, wa, side, half, width, window, levels, total_count = sizes
     own = 2 * half
     li, ri, wi = lax.axis_index("lb"), lax.axis_index("rb"), lax.axis_index("wa")
@@ -105,20 +105,25 @@
     mine = ri * 2 + wi
     chunks = 2 * rb
     own_column = chunks + li
-    xs = [lax.rem(xi + step, side) for step in range(side)]
-    ys = [lax.rem(yi + step, side) for step in range(side)]
+    first_at, second_at = xi + wi * (yi - xi), yi + wi * (xi - yi)
+    first_unit, second_unit = side - wi * (side - 1), 1 + wi * (side - 1)
+    firsts = [lax.rem(first_at + step, side) for step in range(side)]
+    seconds = [lax.rem(second_at + step, side) for step in range(side)]
     zs = [lax.rem(li + step, lb) for step in range(lb)]
-    plane_steps = sorted(
-        range(1, rb),
-        key=lambda step: -min(step // side, side - step // side) - min(step % side, side - step % side),
-    )
+    ring_steps = sorted(range(1, side), key=lambda step: min(step, side - step))
+    relay_steps = [(step, 0) for step in ring_steps]
+    later_steps = [(a, b) for a in [0] + ring_steps for b in ring_steps]
+    arrivals = relay_steps + later_steps
     column_steps = sorted(range(1, lb), key=lambda step: -min(step, lb - step))
 
-    def plane_peer(step):
-        return xs[step // side] * side + ys[step % side]
-
-    def plane_source(step):
-        return xs[-(step // side) % side] * side + ys[-(step % side) % side]
+    def plane_peer(a, b):
+        return firsts[a] * first_unit + seconds[b] * second_unit
+
+    def plane_source(a, b):
+        return firsts[-a % side] * first_unit + seconds[-b % side] * second_unit
+
+    def other_source(a, b):
+        return seconds[-a % side] * second_unit + firsts[-b % side] * first_unit
 
     for steps, held, first in ((FAR, lv_far, 0), (NEAR, lv_near, len(FAR))):
         for place, step in enumerate(steps):
@@ -128,8 +133,8 @@
 
     barrier = pltpu.get_barrier_semaphore()
 
-    for step in plane_steps:
-        pl.semaphore_signal(barrier, inc=1, device_id={"rb": plane_peer(step)}, device_id_type=MESH)
+    for a, b in arrivals:
+        pl.semaphore_signal(barrier, inc=1, device_id={"rb": plane_peer(a, b)}, device_id_type=MESH)
     for step in range(lb):
         for turn in range(2):
             if step or turn:
@@ -138,13 +143,20 @@
                     device_id={"lb": zs[step], "wa": other if turn else wi}, device_id_type=MESH,
                 )
 
+    def plane_send(number, source, buf, slot, place, a, b):
+        pltpu.make_async_remote_copy(
+            src_ref=source, dst_ref=buf.at[slot],
+            send_sem=gather_send.at[number], recv_sem=gather_recv.at[number, place],
+            device_id={"rb": plane_peer(a, b)}, device_id_type=MESH,
+        ).start()
+
     def gather_start(number, source, buf):
-        for step in plane_steps:
-            pltpu.make_async_remote_copy(
-                src_ref=source, dst_ref=buf.at[mine],
-                send_sem=gather_send.at[number], recv_sem=gather_recv.at[number, step],
-                device_id={"rb": plane_peer(step)}, device_id_type=MESH,
-            ).start()
+        for step in ring_steps:
+            plane_send(number, source, buf, mine, step * side, step, 0)
+        for step in ring_steps:
+            plane_send(number, source, buf, mine, step, 0, step)
+
+    def column_start(number, source, buf):
         for step in column_steps:
             pltpu.make_async_remote_copy(
                 src_ref=source, dst_ref=buf.at[own_column],
@@ -152,21 +164,38 @@
                 device_id={"lb": zs[step]}, device_id_type=MESH,
             ).start()
 
-    def forward(number, source, buf, slot):
+    def forward(number, source, buf, slot, step):
         pltpu.make_async_remote_copy(
             src_ref=source, dst_ref=buf.at[slot],
-            send_sem=fwd_send.at[number], recv_sem=fwd_recv.at[number],
+            send_sem=fwd_send.at[number], recv_sem=fwd_recv.at[number, step],
             device_id={"wa": other}, device_id_type=MESH,
         ).start()
 
+    def gather_relay(number, buf):
+        for a, _ in relay_steps:
+            slot = plane_source(a, 0) * 2 + wi
+            wait_bytes(buf.at[slot], gather_recv.at[number, a * side])
+            for step in ring_steps:
+                plane_send(number, buf.at[slot], buf, slot, a * side + step, 0, step)
+            forward(number, buf.at[slot], buf, slot, a * side)
+
     def gather_forward(number, buf, steps):
-        for step in steps:
-            slot = plane_source(step) * 2 + wi
-            wait_bytes(buf.at[slot], gather_recv.at[number, step])
-            forward(number, buf.at[slot], buf, slot)
-
-    def gather_finish(number, buf, count):
-        wait_bytes(buf.at[pl.ds(0, count)], fwd_recv.at[number])
+        for a, b in steps:
+            slot = plane_source(a, b) * 2 + wi
+            wait_bytes(buf.at[slot], gather_recv.at[number, a * side + b])
+            forward(number, buf.at[slot], buf, slot, a * side + b)
+
+    def gather_finish(number, buf):
+        for a, b in arrivals:
+            wait_bytes(buf.at[other_source(a, b) * 2 + other], fwd_recv.at[number, a * side + b])
+
+    def pick(values, index):
+        found = values[0]
+        for place in range(1, len(values)):
+            found = jnp.where(index == place, values[place], found)
+        return found
+
+    def column_finish(number, buf):
         wait_bytes(buf.at[pl.ds(0, lb - 1)], column_recv.at[number])
 
     def gather_drain(number, buf, count):
@@ -223,6 +252,7 @@
     lax.fori_loop(0, joint_steps // 2, joint_body, 0)
     pl.semaphore_wait(barrier, rb - 1 + 2 * lb - 1)
     gather_start(0, x.at[0, mine], x.at[0])
+    column_start(0, x.at[0, mine], x.at[0])
     lax.fori_loop(joint_steps // 2, joint_steps, joint_body, 0)
 
     eye = lax.broadcasted_iota(jnp.int32, (window, window), 0) == lax.broadcasted_iota(
@@ -256,18 +286,31 @@
         entries = entries + jnp.where(lane == wi * (levels // 2) + level, column, 0.0)
     dl_mine[...] = entries.astype(jnp.bfloat16)
     swap_diag = pltpu.make_async_remote_copy(
-        src_ref=dl_mine, dst_ref=dl_swap, send_sem=out_send.at[2], recv_sem=out_recv.at[2],
+        src_ref=dl_mine, dst_ref=dl_swap, send_sem=diag_sem.at[0], recv_sem=diag_sem.at[1],
         device_id={"wa": other}, device_id_type=MESH,
     )
     swap_diag.start()
-    gather_forward(0, x.at[0], plane_steps)
+    gather_relay(0, x.at[0])
+    gather_forward(0, x.at[0], later_steps)
     swap_diag.wait()
     both = (dl_mine[...].astype(jnp.float32) + dl_swap[...].astype(jnp.float32)).astype(jnp.bfloat16)
     dl_all[ri * 2] = both[:half]
     dl_all[ri * 2 + 1] = both[half:]
     dl_all[own_column] = dl_all[mine]
     gather_start(1, dl_all.at[mine], dl_all)
-    gather_finish(0, x.at[0], rb - 1)
+    column_start(1, dl_all.at[mine], dl_all)
+    gather_finish(0, x.at[0])
+
+    def correct(k, chunk, carry):
+        for start in range(0, half, 16):
+            span = pl.ds(start, 16)
+            residual = jnp.zeros((16, width), jnp.float32)
+            for i in range(k + 1):
+                residual = residual + tiled(coef[i], 16, width) * y[i, chunk, span].astype(jnp.float32)
+                residual = residual + tiled(coef[4 + i], 16, width) * x[i, chunk, span].astype(jnp.float32)
+            below = jnp.abs(diag[chunk, span] - tiled(coef[8], 16, width)) + 1.0
+            x[k + 1, chunk, span] = (residual / below).astype(jnp.bfloat16)
+        return carry
 
     gram, cross, mix = {}, {}, {}
     for k in range(ITERS + 1):
@@ -325,6 +368,12 @@
         far_swap = swap_copy(0, far_out, far_in)
         far_swap.start()
         left_product(lv_near, z_near, 0, held_levels // 2)
+        if k == 0:
+            column_finish(0, x.at[0])
+            gather_relay(1, dl_all)
+        else:
+            column_finish(1 + k, y.at[k - 1])
+            lax.fori_loop(chunks, chunks + lb, functools.partial(correct, k - 1), 0)
         far_swap.wait()
         for place in range(len(FAR)):
             total = part_far[place, wi] + far_in[place].astype(jnp.float32)
@@ -344,7 +393,7 @@
         near_swap = swap_copy(1, near_out, near_in)
         near_swap.start()
         if k == 0:
-            gather_forward(1, dl_all, plane_steps)
+            gather_forward(1, dl_all, later_steps)
         near_swap.wait()
         for place in range(2, 4):
             total = part_near[place, wi] + near_in[place].astype(jnp.float32)
@@ -356,11 +405,11 @@
         lines += [folded(sums) for sums in cross_sums]
         lines += [jnp.zeros((1, 128), jnp.float32)] * (8 - len(lines))
         sc_xy[k, ri] = jnp.concatenate(lines, axis=0)
-        for step in plane_steps:
+        for a, b in reversed(arrivals):
             pltpu.make_async_remote_copy(
                 src_ref=sc_xy.at[k, ri], dst_ref=sc_xy.at[k, ri],
                 send_sem=xy_send.at[k], recv_sem=xy_recv.at[k],
-                device_id={"rb": plane_peer(step)}, device_id_type=MESH,
+                device_id={"rb": plane_peer(a, b)}, device_id_type=MESH,
             ).start()
         wait_bytes(relay_in, relay_recv.at[k])
         wait_bytes(relay4_in, relay4_recv.at[k])
@@ -397,18 +446,27 @@
         wait_bytes(rs_in, rs_recv.at[k])
         for place in range(4):
             image = image + rs_in[place].astype(jnp.float32)
-        y_own[k] = image
+        y_own[k, wi] = image
+        pltpu.make_async_remote_copy(
+            src_ref=y_own.at[k, wi], dst_ref=y_own.at[k, wi],
+            send_sem=own_send.at[k], recv_sem=own_recv.at[k],
+            device_id={"wa": other}, device_id_type=MESH,
+        ).start()
         if k < ITERS:
             rounded = image.astype(jnp.bfloat16)
             y[k, mine] = rounded
             y[k, own_column] = rounded
             gather_start(2 + k, y.at[k, mine], y.at[k])
-            forward(2 + k, y.at[k, mine], y.at[k], mine)
+            forward(2 + k, y.at[k, mine], y.at[k], mine, 0)
             share_sums()
+            column_start(2 + k, y.at[k, mine], y.at[k])
         wait_bytes(rs_out, rs_send.at[k])
         wait_bytes(relay_out, relay_send.at[k])
+        if k < ITERS:
+            gather_relay(2 + k, y.at[k])
         if k == 0:
-            gather_finish(1, dl_all, rb - 1)
+            gather_finish(1, dl_all)
+            column_finish(1, dl_all)
             rest = level_ref[...]
             found = jnp.zeros(((chunks + lb) * half, width), jnp.float32)
             for _ in range(3):
@@ -418,9 +476,12 @@
                     dl_all[...].reshape((chunks + lb) * half, 128), term, preferred_element_type=jnp.float32
                 )
             diag[...] = found.reshape(chunks + lb, half, width)
-        early = len(plane_steps) // 2
+        places = [0] + [a * side + b for a, b in arrivals]
+        sources = [ri] + [plane_source(a, b) for a, b in arrivals]
+        other_sources = [ri] + [other_source(a, b) for a, b in arrivals]
+        early = 1 + len(relay_steps) + len(ring_steps)
         if k < ITERS:
-            gather_forward(2 + k, y.at[k], plane_steps[:early])
+            gather_forward(2 + k, y.at[k], arrivals[len(relay_steps) : early - 1])
         wait_bytes(sc_z.at[k, pl.ds(0, 2 * lb - 1)], z_recv.at[k])
         total = sc_z[k, 0]
         for j in range(1, 2 * lb):
@@ -458,44 +519,39 @@
         coef[8] = theta
 
         if k < ITERS:
-            gather_forward(2 + k, y.at[k], plane_steps[early:])
-            gather_finish(2 + k, y.at[k], rb)
-
-            def correct(chunk, carry):
-                for start in range(0, half, 16):
-                    span = pl.ds(start, 16)
-                    ritz = tiled(coef[8], 16, width)
-                    residual = jnp.zeros((16, width), jnp.float32)
-                    for i in range(k + 1):
-                        residual = residual + tiled(coef[i], 16, width) * y[i, chunk, span].astype(jnp.float32)
-                        residual = residual + tiled(coef[4 + i], 16, width) * x[i, chunk, span].astype(jnp.float32)
-                    below = jnp.abs(diag[chunk, span] - ritz) + 1.0
-                    x[k + 1, chunk, span] = (residual / below).astype(jnp.bfloat16)
-                return carry
-
-            lax.fori_loop(0, chunks + lb, correct, 0)
-
-    ritz_rows = jnp.zeros((half, width), jnp.float32)
-    image_rows = jnp.zeros((half, width), jnp.float32)
-    for i in range(ITERS + 1):
-        alpha = tiled(coef[i], half, width)
-        ritz_rows = ritz_rows + alpha * x[i, mine].astype(jnp.float32)
-        image_rows = image_rows + alpha * y_own[i]
-    image_rows = image_rows - tiled(coef[8], half, width) * ritz_rows
-    my_rows = pl.ds(pl.multiple_of(wi * half, half), half)
-    copies = []
-    for n, (ref, rows) in enumerate(((ritz_ref, ritz_rows), (residual_ref, image_rows))):
+
+            def correct_early(index, carry):
+                return correct(k, pick(sources, index) * 2 + wi, carry)
+
+            def correct_late(index, carry):
+                slot, step = pick(sources, index) * 2 + wi, pick(places, index)
+                wait_bytes(y.at[k, slot], gather_recv.at[2 + k, step])
+                forward(2 + k, y.at[k, slot], y.at[k], slot, step)
+                return correct(k, slot, carry)
+
+            def correct_other(index, carry):
+                slot, step = pick(other_sources, index) * 2 + other, pick(places, index)
+                wait_bytes(y.at[k, slot], fwd_recv.at[2 + k, step])
+                return correct(k, slot, carry)
+
+            lax.fori_loop(0, early, correct_early, 0)
+            lax.fori_loop(early, rb, correct_late, 0)
+            lax.fori_loop(0, rb, correct_other, 0)
+
+    for k in range(ITERS + 1):
+        wait_bytes(y_own.at[k, other], own_recv.at[k])
+    theta_rows = tiled(coef[8], half, width)
+    for h in range(2):
+        ritz_rows = jnp.zeros((half, width), jnp.float32)
+        image_rows = jnp.zeros((half, width), jnp.float32)
+        for i in range(ITERS + 1):
+            alpha = tiled(coef[i], half, width)
+            ritz_rows = ritz_rows + alpha * x[i, ri * 2 + h].astype(jnp.float32)
+            image_rows = image_rows + alpha * y_own[i, h]
+        image_rows = image_rows - theta_rows * ritz_rows
         for s in range(physical):
-            ref[my_rows, s, :] = rows[:, s * window : (s + 1) * window]
-        copies.append(
-            pltpu.make_async_remote_copy(
-                src_ref=ref.at[my_rows], dst_ref=ref.at[my_rows],
-                send_sem=out_send.at[n], recv_sem=out_recv.at[n],
-                device_id={"wa": other}, device_id_type=MESH,
-            )
-        )
-    for copy in copies:
-        copy.start()
+            ritz_ref[h * half : (h + 1) * half, s, :] = ritz_rows[:, s * window : (s + 1) * window]
+            residual_ref[h * half : (h + 1) * half, s, :] = image_rows[:, s * window : (s + 1) * window]
     gather_drain(0, x.at[0], rb - 1)
     gather_drain(1, dl_all, rb - 1)
     for k in range(ITERS):
@@ -505,8 +561,12 @@
         wait_bytes(sc_xy.at[k, pl.ds(0, rb - 1)], xy_send.at[k])
     for k in range(ITERS + 1):
         wait_bytes(sc_z.at[k, pl.ds(0, 2 * lb - 1)], z_send.at[k])
-    for copy in copies:
-        copy.wait()
+        wait_bytes(y_own.at[k, wi], own_send.at[k])
+
+
+def copy_kernel(first_in, second_in, first_out, second_out):
+    first_out[...] = first_in[...]
+    second_out[...] = second_in[...]
 
 
 def per_device(initial_guess, left_environment, right_environment, operator_blocks, operator_pairs):
@@ -545,7 +605,7 @@
             pltpu.VMEM((local_levels, len(NEAR), own, depth), bf16),
             pltpu.VMEM((n, 2 * rb + lb, half, width), bf16),
             pltpu.VMEM((ITERS, 2 * rb + lb, half, width), bf16),
-            pltpu.VMEM((n, half, width), f32),
+            pltpu.VMEM((n, 2, half, width), f32),
             pltpu.VMEM((len(FAR) * own, local_levels * width), bf16),
             pltpu.VMEM((len(NEAR) * own, local_levels * width), bf16),
             pltpu.VMEM((len(FAR), 2, half, width), f32),
@@ -570,9 +630,9 @@
             DMA((2 + ITERS,)),
             DMA((2 + ITERS, rb)),
             DMA((2 + ITERS,)),
+            DMA((2 + ITERS, rb)),
             DMA((2 + ITERS,)),
             DMA((2 + ITERS,)),
-            DMA((2 + ITERS,)),
             DMA((n,)),
             DMA((n,)),
             DMA((n,)),
@@ -584,8 +644,9 @@
             DMA((n,)),
             DMA((n,)),
             DMA((n,)),
-            DMA((3,)),
-            DMA((3,)),
+            DMA((n,)),
+            DMA((n,)),
+            DMA((2,)),
         ],
         compiler_params=pltpu.CompilerParams(
             collective_id=0, has_side_effects=True, vmem_limit_bytes=60 * 1024 * 1024
@@ -594,7 +655,12 @@
         initial_guess, left, right_environment,
         jnp.transpose(operator_blocks, (1, 2, 0)), jnp.transpose(operator_pairs),
     )
-    return ritz, residual
+    return pl.pallas_call(
+        copy_kernel,
+        out_shape=[jax.ShapeDtypeStruct((own, physical, window), f32)] * 2,
+        in_specs=[vmem, vmem],
+        out_specs=[vmem, vmem],
+    )(ritz, residual)
 
 
 def solution(mesh):

time: 118 us -> 110 us (0.932)
  Pallas kernels: 114 us -> 109 us
  local copies, waits for them, and re-layouts: 3.14 us -> 0 us
    pallas_call x1, Pallas kernels: 114 us -> 108 us  [per_device(): pl.pallas_call(functools.partial(davidson_kernel, sizes), out_shape=[jax....]
    unnamed x2 -> x0, local copies, waits for them, and re-layouts: 3.14 us -> none
    pallas_call x0 -> x1, Pallas kernels: none -> 1.68 us  [per_device(): pl.pallas_call(copy_kernel, out_shape=[jax.ShapeDtypeStruct((own, physica...]
where the time goes in v2:
time: 110 us
  Pallas kernels  109 us (99%)
    pallas_call x1, Pallas kernels, per_device(): pl.pallas_call(functools.partial(davidson_kernel, sizes), out_shape=[jax....  108 us

profile of v2, /device:TPU:1, one launch (start us, length us, event | category | flops | bytes accessed | tf_op | source)
XLA Modules:
  0.0 110.1 jit_solution(6671506349426449698)
XLA Ops:
  0.6 107.8 %shard_map.68 = (f32[64,4,128]{2,1,0:T(4,128)}, f32[64,4,128]{2,1,0:T(4,128)}) custom-call(bf16[64,4,128]{2,1,0:T(4,128)(2,1)} %guess_ref.1, bf16[4,8,64,1024]{3,2,1,0:T(8,128)(2,1)} %bitcast.3, bf16[128,8,128]{2,1,0:T(8,128)(2,1)} %right_ref.1, f32[4,4,16]{2,1,0:T(4,128)} %bitcast.4, s32[2,16]{1,0:T(2,128)} %bitcast.5), custom_call_target="tpu_custom_call" | custom-call | tf_op jit(solution)/shard_map/pallas_call | solution.py:591
  108.4 1.7 %shard_map.69 = (f32[64,4,128]{2,1,0:T(4,128)}, f32[64,4,128]{2,1,0:T(4,128)}) custom-call(f32[64,4,128]{2,1,0:T(4,128)} %get-tuple-element.4.first_in, f32[64,4,128]{2,1,0:T(4,128)} %get-tuple-element.5.second_in), custom_call_target="tpu_custom_call" | custom-call | tf_op jit(solution)/shard_map/pallas_call | solution.py:658

commit v3 on v2

--- a/solution.py
+++ b/solution.py
@@ -105,25 +105,20 @@
     mine = ri * 2 + wi
     chunks = 2 * rb
     own_column = chunks + li
-    first_at, second_at = xi + wi * (yi - xi), yi + wi * (xi - yi)
-    first_unit, second_unit = side - wi * (side - 1), 1 + wi * (side - 1)
-    firsts = [lax.rem(first_at + step, side) for step in range(side)]
-    seconds = [lax.rem(second_at + step, side) for step in range(side)]
+    xs = [lax.rem(xi + step, side) for step in range(side)]
+    ys = [lax.rem(yi + step, side) for step in range(side)]
     zs = [lax.rem(li + step, lb) for step in range(lb)]
-    ring_steps = sorted(range(1, side), key=lambda step: min(step, side - step))
-    relay_steps = [(step, 0) for step in ring_steps]
-    later_steps = [(a, b) for a in [0] + ring_steps for b in ring_steps]
-    arrivals = relay_steps + later_steps
+    plane_steps = sorted(
+        range(1, rb),
+        key=lambda step: -min(step // side, side - step // side) - min(step % side, side - step % side),
+    )
     column_steps = sorted(range(1, lb), key=lambda step: -min(step, lb - step))
 
-    def plane_peer(a, b):
-        return firsts[a] * first_unit + seconds[b] * second_unit
-
-    def plane_source(a, b):
-        return firsts[-a % side] * first_unit + seconds[-b % side] * second_unit
-
-    def other_source(a, b):
-        return seconds[-a % side] * second_unit + firsts[-b % side] * first_unit
+    def plane_peer(step):
+        return xs[step // side] * side + ys[step % side]
+
+    def plane_source(step):
+        return xs[-(step // side) % side] * side + ys[-(step % side) % side]
 
     for steps, held, first in ((FAR, lv_far, 0), (NEAR, lv_near, len(FAR))):
         for place, step in enumerate(steps):
@@ -133,8 +128,8 @@
 
     barrier = pltpu.get_barrier_semaphore()
 
-    for a, b in arrivals:
-        pl.semaphore_signal(barrier, inc=1, device_id={"rb": plane_peer(a, b)}, device_id_type=MESH)
+    for step in plane_steps:
+        pl.semaphore_signal(barrier, inc=1, device_id={"rb": plane_peer(step)}, device_id_type=MESH)
     for step in range(lb):
         for turn in range(2):
             if step or turn:
@@ -143,18 +138,13 @@
                     device_id={"lb": zs[step], "wa": other if turn else wi}, device_id_type=MESH,
                 )
 
-    def plane_send(number, source, buf, slot, place, a, b):
-        pltpu.make_async_remote_copy(
-            src_ref=source, dst_ref=buf.at[slot],
-            send_sem=gather_send.at[number], recv_sem=gather_recv.at[number, place],
-            device_id={"rb": plane_peer(a, b)}, device_id_type=MESH,
-        ).start()
-
     def gather_start(number, source, buf):
-        for step in ring_steps:
-            plane_send(number, source, buf, mine, step * side, step, 0)
-        for step in ring_steps:
-            plane_send(number, source, buf, mine, step, 0, step)
+        for step in plane_steps:
+            pltpu.make_async_remote_copy(
+                src_ref=source, dst_ref=buf.at[mine],
+                send_sem=gather_send.at[number], recv_sem=gather_recv.at[number, step],
+                device_id={"rb": plane_peer(step)}, device_id_type=MESH,
+            ).start()
 
     def column_start(number, source, buf):
         for step in column_steps:
@@ -171,23 +161,15 @@
             device_id={"wa": other}, device_id_type=MESH,
         ).start()
 
-    def gather_relay(number, buf):
-        for a, _ in relay_steps:
-            slot = plane_source(a, 0) * 2 + wi
-            wait_bytes(buf.at[slot], gather_recv.at[number, a * side])
-            for step in ring_steps:
-                plane_send(number, buf.at[slot], buf, slot, a * side + step, 0, step)
-            forward(number, buf.at[slot], buf, slot, a * side)
-
     def gather_forward(number, buf, steps):
-        for a, b in steps:
-            slot = plane_source(a, b) * 2 + wi
-            wait_bytes(buf.at[slot], gather_recv.at[number, a * side + b])
-            forward(number, buf.at[slot], buf, slot, a * side + b)
+        for step in steps:
+            slot = plane_source(step) * 2 + wi
+            wait_bytes(buf.at[slot], gather_recv.at[number, step])
+            forward(number, buf.at[slot], buf, slot, step)
 
     def gather_finish(number, buf):
-        for a, b in arrivals:
-            wait_bytes(buf.at[other_source(a, b) * 2 + other], fwd_recv.at[number, a * side + b])
+        for step in plane_steps:
+            wait_bytes(buf.at[plane_source(step) * 2 + other], fwd_recv.at[number, step])
 
     def pick(values, index):
         found = values[0]
@@ -249,11 +231,11 @@
         return carry
 
     joint_steps = (levels // 2) * (window // chunk_rows)
-    lax.fori_loop(0, joint_steps // 2, joint_body, 0)
+    lax.fori_loop(0, joint_steps // 4, joint_body, 0)
     pl.semaphore_wait(barrier, rb - 1 + 2 * lb - 1)
     gather_start(0, x.at[0, mine], x.at[0])
     column_start(0, x.at[0, mine], x.at[0])
-    lax.fori_loop(joint_steps // 2, joint_steps, joint_body, 0)
+    lax.fori_loop(joint_steps // 4, joint_steps, joint_body, 0)
 
     eye = lax.broadcasted_iota(jnp.int32, (window, window), 0) == lax.broadcasted_iota(
         jnp.int32, (window, window), 1
@@ -290,8 +272,7 @@
         device_id={"wa": other}, device_id_type=MESH,
     )
     swap_diag.start()
-    gather_relay(0, x.at[0])
-    gather_forward(0, x.at[0], later_steps)
+    gather_forward(0, x.at[0], plane_steps)
     swap_diag.wait()
     both = (dl_mine[...].astype(jnp.float32) + dl_swap[...].astype(jnp.float32)).astype(jnp.bfloat16)
     dl_all[ri * 2] = both[:half]
@@ -370,7 +351,6 @@
         left_product(lv_near, z_near, 0, held_levels // 2)
         if k == 0:
             column_finish(0, x.at[0])
-            gather_relay(1, dl_all)
         else:
             column_finish(1 + k, y.at[k - 1])
             lax.fori_loop(chunks, chunks + lb, functools.partial(correct, k - 1), 0)
@@ -393,35 +373,39 @@
         near_swap = swap_copy(1, near_out, near_in)
         near_swap.start()
         if k == 0:
-            gather_forward(1, dl_all, later_steps)
+            gather_forward(1, dl_all, plane_steps)
         near_swap.wait()
-        for place in range(2, 4):
-            total = part_near[place, wi] + near_in[place].astype(jnp.float32)
-            rs_out[place] = total.astype(jnp.bfloat16)
-            along(rs_out.at[place], rs_in.at[place], rs_send.at[k], rs_recv.at[k], NEAR[place])
+        def send_near():
+            wait_bytes(relay_in, relay_recv.at[k])
+            wait_bytes(relay4_in, relay4_recv.at[k])
+            for place in range(4):
+                total = part_near[place, wi] + near_in[place].astype(jnp.float32)
+                if place < 2:
+                    total = total + relay_in[place].astype(jnp.float32)
+                    extra = relay4_in[place].astype(jnp.float32)
+                    total = jnp.concatenate(
+                        [total[:16] + extra, total[16:]] if place == 0 else [total[:16], total[16:] + extra],
+                        axis=0,
+                    )
+                rs_out[place] = total.astype(jnp.bfloat16)
+                along(rs_out.at[place], rs_in.at[place], rs_send.at[k], rs_recv.at[k], NEAR[place])
+
+        if k < ITERS:
+            send_near()
         for place, step in enumerate(NEAR):
             total = part_near[place, wi] + near_in[place].astype(jnp.float32)
             cross_sums = add_cross(cross_sums, total, step)
         lines += [folded(sums) for sums in cross_sums]
         lines += [jnp.zeros((1, 128), jnp.float32)] * (8 - len(lines))
         sc_xy[k, ri] = jnp.concatenate(lines, axis=0)
-        for a, b in reversed(arrivals):
+        for step in plane_steps:
             pltpu.make_async_remote_copy(
                 src_ref=sc_xy.at[k, ri], dst_ref=sc_xy.at[k, ri],
                 send_sem=xy_send.at[k], recv_sem=xy_recv.at[k],
-                device_id={"rb": plane_peer(a, b)}, device_id_type=MESH,
+                device_id={"rb": plane_peer(step)}, device_id_type=MESH,
             ).start()
-        wait_bytes(relay_in, relay_recv.at[k])
-        wait_bytes(relay4_in, relay4_recv.at[k])
-        for place in range(2):
-            total = part_near[place, wi] + near_in[place].astype(jnp.float32)
-            total = total + relay_in[place].astype(jnp.float32)
-            extra = relay4_in[place].astype(jnp.float32)
-            total = jnp.concatenate(
-                [total[:16] + extra, total[16:]] if place == 0 else [total[:16], total[16:] + extra], axis=0
-            )
-            rs_out[place] = total.astype(jnp.bfloat16)
-            along(rs_out.at[place], rs_in.at[place], rs_send.at[k], rs_recv.at[k], NEAR[place])
+        if k == ITERS:
+            send_near()
 
         def share_sums():
             wait_bytes(sc_xy.at[k, pl.ds(0, rb - 1)], xy_recv.at[k])
@@ -462,8 +446,6 @@
             column_start(2 + k, y.at[k, mine], y.at[k])
         wait_bytes(rs_out, rs_send.at[k])
         wait_bytes(relay_out, relay_send.at[k])
-        if k < ITERS:
-            gather_relay(2 + k, y.at[k])
         if k == 0:
             gather_finish(1, dl_all)
             column_finish(1, dl_all)
@@ -476,12 +458,11 @@
                     dl_all[...].reshape((chunks + lb) * half, 128), term, preferred_element_type=jnp.float32
                 )
             diag[...] = found.reshape(chunks + lb, half, width)
-        places = [0] + [a * side + b for a, b in arrivals]
-        sources = [ri] + [plane_source(a, b) for a, b in arrivals]
-        other_sources = [ri] + [other_source(a, b) for a, b in arrivals]
-        early = 1 + len(relay_steps) + len(ring_steps)
+        arrivals = [0] + plane_steps
+        sources = [ri] + [plane_source(step) for step in plane_steps]
+        early = 4
         if k < ITERS:
-            gather_forward(2 + k, y.at[k], arrivals[len(relay_steps) : early - 1])
+            gather_forward(2 + k, y.at[k], arrivals[1:early])
         wait_bytes(sc_z.at[k, pl.ds(0, 2 * lb - 1)], z_recv.at[k])
         total = sc_z[k, 0]
         for j in range(1, 2 * lb):
@@ -524,13 +505,13 @@
                 return correct(k, pick(sources, index) * 2 + wi, carry)
 
             def correct_late(index, carry):
-                slot, step = pick(sources, index) * 2 + wi, pick(places, index)
+                slot, step = pick(sources, index) * 2 + wi, pick(arrivals, index)
                 wait_bytes(y.at[k, slot], gather_recv.at[2 + k, step])
                 forward(2 + k, y.at[k, slot], y.at[k], slot, step)
                 return correct(k, slot, carry)
 
             def correct_other(index, carry):
-                slot, step = pick(other_sources, index) * 2 + other, pick(places, index)
+                slot, step = pick(sources, index) * 2 + other, pick(arrivals, index)
                 wait_bytes(y.at[k, slot], fwd_recv.at[2 + k, step])
                 return correct(k, slot, carry)
 

time: 110 us -> 103 us (0.936)
  Pallas kernels: 109 us -> 102 us
    pallas_call x1, Pallas kernels: 108 us -> 101 us  [per_device(): pl.pallas_call(functools.partial(davidson_kernel, sizes), out_shape=[jax....]
where the time goes in v3:
time: 103 us
  Pallas kernels  102 us (99%)
    pallas_call x1, Pallas kernels, per_device(): pl.pallas_call(functools.partial(davidson_kernel, sizes), out_shape=[jax....  101 us

profile of v3, /device:TPU:1, one launch (start us, length us, event | category | flops | bytes accessed | tf_op | source)
XLA Modules:
  0.0 102.8 jit_solution(15634033597584373766)
XLA Ops:
  0.6 100.5 %shard_map.68 = (f32[64,4,128]{2,1,0:T(4,128)}, f32[64,4,128]{2,1,0:T(4,128)}) custom-call(bf16[64,4,128]{2,1,0:T(4,128)(2,1)} %guess_ref.1, bf16[4,8,64,1024]{3,2,1,0:T(8,128)(2,1)} %bitcast.3, bf16[128,8,128]{2,1,0:T(8,128)(2,1)} %right_ref.1, f32[4,4,16]{2,1,0:T(4,128)} %bitcast.4, s32[2,16]{1,0:T(2,128)} %bitcast.5), custom_call_target="tpu_custom_call" | custom-call | tf_op jit(solution)/shard_map/pallas_call | solution.py:572
  101.2 1.7 %shard_map.69 = (f32[64,4,128]{2,1,0:T(4,128)}, f32[64,4,128]{2,1,0:T(4,128)}) custom-call(f32[64,4,128]{2,1,0:T(4,128)} %get-tuple-element.4.first_in, f32[64,4,128]{2,1,0:T(4,128)} %get-tuple-element.5.second_in), custom_call_target="tpu_custom_call" | custom-call | tf_op jit(solution)/shard_map/pallas_call | solution.py:639

commit v4 on v3

--- a/solution.py
+++ b/solution.py
@@ -170,6 +170,10 @@
     def gather_finish(number, buf):
         for step in plane_steps:
             wait_bytes(buf.at[plane_source(step) * 2 + other], fwd_recv.at[number, step])
+
+    def source_of(step):
+        a, b = lax.div(step, side), lax.rem(step, side)
+        return lax.rem(xi + side - a, side) * side + lax.rem(yi + side - b, side)
 
     def pick(values, index):
         found = values[0]
@@ -459,10 +463,6 @@
                 )
             diag[...] = found.reshape(chunks + lb, half, width)
         arrivals = [0] + plane_steps
-        sources = [ri] + [plane_source(step) for step in plane_steps]
-        early = 4
-        if k < ITERS:
-            gather_forward(2 + k, y.at[k], arrivals[1:early])
         wait_bytes(sc_z.at[k, pl.ds(0, 2 * lb - 1)], z_recv.at[k])
         total = sc_z[k, 0]
         for j in range(1, 2 * lb):
@@ -501,22 +501,21 @@
 
         if k < ITERS:
 
-            def correct_early(index, carry):
-                return correct(k, pick(sources, index) * 2 + wi, carry)
-
             def correct_late(index, carry):
-                slot, step = pick(sources, index) * 2 + wi, pick(arrivals, index)
+                step = pick(arrivals, index)
+                slot = source_of(step) * 2 + wi
                 wait_bytes(y.at[k, slot], gather_recv.at[2 + k, step])
                 forward(2 + k, y.at[k, slot], y.at[k], slot, step)
                 return correct(k, slot, carry)
 
             def correct_other(index, carry):
-                slot, step = pick(sources, index) * 2 + other, pick(arrivals, index)
+                step = pick(arrivals, index)
+                slot = source_of(step) * 2 + other
                 wait_bytes(y.at[k, slot], fwd_recv.at[2 + k, step])
                 return correct(k, slot, carry)
 
-            lax.fori_loop(0, early, correct_early, 0)
-            lax.fori_loop(early, rb, correct_late, 0)
+            correct(k, mine, 0)
+            lax.fori_loop(1, rb, correct_late, 0)
             lax.fori_loop(0, rb, correct_other, 0)
 
     for k in range(ITERS + 1):

time: 103 us -> 103 us (level)
  no operation moved by 1% of the time
where the time goes in v4:
time: 103 us
  Pallas kernels  102 us (99%)
    pallas_call x1, Pallas kernels, per_device(): pl.pallas_call(functools.partial(davidson_kernel, sizes), out_shape=[jax....  100 us

profile of v4, /device:TPU:1, one launch (start us, length us, event | category | flops | bytes accessed | tf_op | source)
XLA Modules:
  0.0 102.7 jit_solution(1770760128506272222)
XLA Ops:
  0.6 100.4 %shard_map.68 = (f32[64,4,128]{2,1,0:T(4,128)}, f32[64,4,128]{2,1,0:T(4,128)}) custom-call(bf16[64,4,128]{2,1,0:T(4,128)(2,1)} %guess_ref.1, bf16[4,8,64,1024]{3,2,1,0:T(8,128)(2,1)} %bitcast.3, bf16[128,8,128]{2,1,0:T(8,128)(2,1)} %right_ref.1, f32[4,4,16]{2,1,0:T(4,128)} %bitcast.4, s32[2,16]{1,0:T(2,128)} %bitcast.5), custom_call_target="tpu_custom_call" | custom-call | tf_op jit(solution)/shard_map/pallas_call | solution.py:571
  101.0 1.7 %shard_map.69 = (f32[64,4,128]{2,1,0:T(4,128)}, f32[64,4,128]{2,1,0:T(4,128)}) custom-call(f32[64,4,128]{2,1,0:T(4,128)} %get-tuple-element.4.first_in, f32[64,4,128]{2,1,0:T(4,128)} %get-tuple-element.5.second_in), custom_call_target="tpu_custom_call" | custom-call | tf_op jit(solution)/shard_map/pallas_call | solution.py:638
